TPU v7x, 32 devices: a whole 2x2x4 slice. The times are simulated.
32 devices in a mesh: section: 8 (over z, y), expert: 4 (over x, core).
Axes of the slice: x: 2, y: 2, z: 4, core: 2. Of those that a mesh axis runs over, the one named last changes fastest.
Arguments:
- grad_out: bfloat16 [8, 512, 3584], P('section', 'expert'), may hold values from -6 to 6
- hidden_act: bfloat16 [8, 512, 1024], P('section', 'expert'), may hold values from -0.29882812 to 0.29882812
- scores: float32 [8, 512, 4], P('section', 'expert'), may hold values from -8 to 8
- expert_ids: int32 [8, 512], P('section', 'expert'), may hold values from 0 to 3, as said below
- slot_ids: int32 [8, 512], P('section', 'expert'), may hold values from 0 to 55, as said below
- counts: int32 [8, 4, 4], P('section'), may hold values from 0 to 56, as said below
- down_weight: bfloat16 [4, 1024, 3584], P('expert'), may hold values from -0.1875 to 0.1875
- router: bfloat16 [4, 3584], replicated, may hold values from -0.8984375 to 0.8984375
Outputs:
- act_grad: bfloat16 [8, 512, 1024], P('section', 'expert')
- score_grad: float32 [8, 512, 4], P('section', 'expert')
- upstream_grad: bfloat16 [8, 512, 3584], P('section', 'expert')
Inputs may be any that keep to these rules, and one draw needn't show every extreme that they name: `expert_ids`: the 128 tokens of one device name each expert at most 56 times; in every section one expert gets exactly 56 tokens from every device. `slot_ids`: a token's slot is the number of earlier tokens of its device that name the same expert. counts[s, e] is at most the number of tokens of device s of the section that name expert e, and may be smaller; routes whose slot is not below it are dropped; for the expert that gets 56 tokens from every device it is 56.
All inputs are finite; a program needn't handle non-finite values.
Results may differ from a plain program's by a relative error of at most 0.009.
Values may be sent and summed in bfloat16 or wider, within the bound.
A program may use at most 64 MiB of HBM per device.

v0:
```python
import functools

import jax
import jax.numpy as jnp
from jax import lax
from jax.experimental import pallas as pl
from jax.experimental.pallas import tpu as pltpu
from jax.sharding import PartitionSpec as P

route_scale = 2.5
MESH = pl.DeviceIdType.MESH
BF = jnp.bfloat16
F32 = jnp.float32


def row_parts(capacity):
    head = capacity // 16 * 16
    if head == capacity and head >= 32:
        head -= 16
    parts = []
    if head > 16:
        parts.append((0, head - 16, head - 16))
    if head:
        parts.append((max(head - 16, 0), head, 16))
    if capacity > head:
        parts.append((head, capacity, -(-(capacity - head) // 8) * 8))
    return parts


def column_cuts(width, pieces):
    while width % (pieces * 128):
        pieces -= 1
    return pieces, width // pieces


def kernel(cfg, grad_hbm, hidden_hbm, logits_hbm, ids_hbm, slots_hbm, counts_hbm, weight_hbm, router_hbm,
           act_ref, score_ref, got, got_slope, router_ref, *rest):
    n, n_section, parts, cuts = cfg["n"], cfg["n_section"], cfg["parts"], cfg["cuts"]
    n_parts = len(parts)
    rest = list(rest)
    take = lambda count: [rest.pop(0) for _ in range(count)]
    grad, hidden, weight, slope_out = take(4)
    logits_ref, ids_ref, slots_ref, counts_ref = take(4)
    sends, recvs, accs, results, returns, hiddens = (take(n_parts) for _ in range(6))
    load_sem, grad_sem, weight_sem, up_sem = take(4)
    send_sems, recv_sems, back_send, back_recv = (take(n_parts) for _ in range(4))

    tok, width = grad.shape
    section = lax.axis_index("section")
    me = lax.axis_index("expert")
    chips = n // 2
    chip, core = me // 2, lax.rem(me, 2)
    target = [2 * lax.rem(chip + k // 2, chips) + lax.rem(core + k % 2, 2) for k in range(n)]
    source = [2 * lax.rem(chip + chips - k // 2, chips) + lax.rem(core + k % 2, 2) for k in range(n)]
    order = [k for k in range(2, n)] + [1]
    has_prev, has_next = section > 0, section < n_section - 1

    pairs = [
        (ids_hbm, ids_ref), (slots_hbm, slots_ref), (counts_hbm.at[0], counts_ref),
        (logits_hbm.at[0], logits_ref), (router_hbm, router_ref), (hidden_hbm.at[0], hidden),
    ]
    loads = [pltpu.make_async_copy(src, dst, load_sem.at[i]) for i, (src, dst) in enumerate(pairs)]
    grad_loads = [
        pltpu.make_async_copy(
            grad_hbm.at[0, :, pl.ds(c * cuts[0][1], cuts[0][1])],
            grad.at[:, pl.ds(c * cuts[0][1], cuts[0][1])],
            grad_sem.at[c],
        )
        for c in range(cuts[0][0])
    ]
    for load in loads[:3] + grad_loads + loads[3:]:
        load.start()
    weight_cuts, weight_cols = cfg["weight_cuts"]
    weight_loads = [
        pltpu.make_async_copy(
            weight_hbm.at[0, :, pl.ds(c * weight_cols, weight_cols)],
            weight.at[:, pl.ds(c * weight_cols, weight_cols)],
            weight_sem.at[c],
        )
        for c in range(weight_cuts)
    ]

    barrier = pltpu.get_barrier_semaphore()
    for k in range(1, n):
        pl.semaphore_signal(barrier, inc=1, device_id=(section, target[k]), device_id_type=MESH)

    @pl.when(has_prev)
    def _():
        pl.semaphore_signal(barrier, inc=1, device_id=(section - 1, me), device_id_type=MESH)

    @pl.when(has_next)
    def _():
        pl.semaphore_signal(barrier, inc=1, device_id=(section + 1, me), device_id_type=MESH)

    for load in loads[:3]:
        load.wait()
    chosen = ids_ref[...]
    places = slots_ref[...]
    limit = jnp.zeros_like(chosen)
    slot_of = jnp.zeros_like(chosen)
    for k in range(n):
        here = chosen == target[k]
        limit = jnp.where(here, counts_ref[me, target[k]], limit)
        slot_of = jnp.where(here, k, slot_of)
    live = places < limit
    picks = []
    for low, high, padded in parts:
        inside = live & (places >= low) & (places < high)
        goal = jnp.where(inside, slot_of * padded + places - low, -1)
        picks.append(lax.broadcasted_iota(jnp.int32, (n * padded, tok), 0) == goal)
    eye = lax.broadcasted_iota(jnp.int32, (tok, tok), 0) == lax.broadcasted_iota(jnp.int32, (tok, tok), 1)

    grad_up = pltpu.make_async_remote_copy(
        src_ref=grad, dst_ref=got, send_sem=up_sem.at[0], recv_sem=up_sem.at[1],
        device_id=(section - 1, me), device_id_type=MESH)

    dispatch = {}
    for p, (low, high, padded) in enumerate(parts):
        count, cols = cuts[p]
        pick = picks[p].astype(BF)
        for c in range(count):
            span = pl.ds(c * cols, cols)
            if p == 0:
                grad_loads[c].wait()
            block = jnp.dot(pick, grad[:, span], preferred_element_type=F32).astype(BF)
            block = block.reshape(n, padded, cols)
            sends[p][:, :, span] = block
            recvs[p][0, :, span] = block[0]
            if not dispatch:
                pl.semaphore_wait(barrier, n - 1 + jnp.where(has_prev, 1, 0) + jnp.where(has_next, 1, 0))
            for k in order:
                copy = pltpu.make_async_remote_copy(
                    src_ref=sends[p].at[k, :, span], dst_ref=recvs[p].at[k, :, span],
                    send_sem=send_sems[p].at[k, c], recv_sem=recv_sems[p].at[k, c],
                    device_id=(section, target[k]), device_id_type=MESH)
                copy.start()
                dispatch[p, c, k] = copy
        if p == 0:

            @pl.when(has_prev)
            def _():
                grad_up.start()

            for load in weight_loads:
                load.start()

    def upright(row):
        return jnp.sum(jnp.where(eye, row, 0), axis=1, keepdims=True)

    for load in loads[3:]:
        load.wait()
    logits = logits_ref[...]
    onehot = chosen == lax.broadcasted_iota(jnp.int32, logits.shape, 0)
    chosen_logit = jnp.sum(jnp.where(onehot, logits, 0.0), axis=0, keepdims=True)
    sigmoid_vals = jax.nn.sigmoid(chosen_logit)
    gate = upright((route_scale * sigmoid_vals).astype(BF).astype(F32))
    for p in range(n_parts):
        hiddens[p][...] = jnp.dot(picks[p].astype(BF), hidden[...], preferred_element_type=F32)

    backs = {}
    weights_waited = 0
    for p, (low, high, padded) in enumerate(parts):
        count, cols = cuts[p]
        rows = n * padded
        for c in range(count):
            while weights_waited * weight_cols < (c + 1) * cols:
                weight_loads[weights_waited].wait()
                weights_waited += 1
            for k in range(1, n):
                dispatch[p, c, k].wait_recv()
            span = pl.ds(c * cols, cols)
            part = lax.dot_general(
                recvs[p][:, :, span].reshape(rows, cols), weight[:, span],
                (((1,), (1,)), ((), ())), preferred_element_type=F32)
            if c:
                part = accs[p][...] + part
            if c < count - 1:
                accs[p][...] = part
        done = part.astype(BF).reshape(n, padded, part.shape[1])
        results[p][...] = done
        returns[p][0] = done[0]
        for k in order:
            copy = pltpu.make_async_remote_copy(
                src_ref=results[p].at[k], dst_ref=returns[p].at[k],
                send_sem=back_send[p].at[k], recv_sem=back_recv[p].at[k],
                device_id=(section, source[k]), device_id_type=MESH)
            copy.start()
            backs[p, k] = copy

    route_grad = jnp.zeros((1, tok), F32)
    for p, (low, high, padded) in enumerate(parts):
        rows = n * padded
        for k in range(1, n):
            backs[p, k].wait_recv()
        own = returns[p][...].reshape(rows, returns[p].shape[2]).astype(F32)
        by_row = jnp.sum(hiddens[p][...] * own, axis=1, keepdims=True)
        route_grad += jnp.sum(jnp.where(picks[p], by_row, 0.0), axis=0, keepdims=True)
    slope = route_grad * route_scale * sigmoid_vals * (1.0 - sigmoid_vals)
    slopes = jnp.where(onehot, slope, 0.0)
    slope_out[...] = slopes
    slope_up = pltpu.make_async_remote_copy(
        src_ref=slope_out, dst_ref=got_slope, send_sem=up_sem.at[2], recv_sem=up_sem.at[3],
        device_id=(section - 1, me), device_id_type=MESH)

    @pl.when(has_prev)
    def _():
        slope_up.start()

    score_ref[0] = slopes
    own_back = None
    for p, (low, high, padded) in enumerate(parts):
        rows = n * padded
        term = lax.dot_general(
            picks[p].astype(BF), returns[p][...].reshape(rows, returns[p].shape[2]),
            (((0,), (0,)), ((), ())), preferred_element_type=F32)
        own_back = term if own_back is None else own_back + term
    act_ref[0] = (gate * own_back).astype(BF)

    for copy in list(dispatch.values()) + list(backs.values()):
        copy.wait_send()

    @pl.when(has_prev)
    def _():
        grad_up.wait_send()

    @pl.when(has_next)
    def _():
        grad_up.wait_recv()
        slope_up.wait_recv()

    @pl.when(has_prev)
    def _():
        slope_up.wait_send()


def finish_kernel(cfg, act_in, score_in, got, got_slope, router_ref, act_out, score_out, up_out, up, sems):
    count, cols = cfg["final_cuts"]
    act_copy = pltpu.make_async_copy(act_in, act_out, sems.at[count])
    score_copy = pltpu.make_async_copy(score_in, score_out, sems.at[count + 1])
    act_copy.start()
    score_copy.start()
    is_last = lax.axis_index("section") == cfg["n_section"] - 1
    scores_bf = got_slope[...].astype(BF)
    copies = []
    for c in range(count):
        span = pl.ds(c * cols, cols)
        term = lax.dot_general(
            scores_bf, router_ref[:, span], (((0,), (0,)), ((), ())), preferred_element_type=F32)
        token_grad = got[:, span].astype(F32) + term
        up[:, span] = jnp.where(is_last, 0.0, token_grad).astype(BF)
        copies.append(pltpu.make_async_copy(up.at[:, span], up_out.at[0, :, span], sems.at[c]))
        copies[-1].start()
    for copy in copies + [act_copy, score_copy]:
        copy.wait()


def on_device(grad_out, hidden_act, scores, expert_ids, slot_ids, counts, down_weight, router):
    n, n_section = lax.axis_size("expert"), lax.axis_size("section")
    _, tok, width = grad_out.shape
    hidden_width = hidden_act.shape[2]
    experts = scores.shape[2]
    capacity = max(2, 7 * tok // (4 * n))
    parts = row_parts(capacity)
    cuts = [column_cuts(width, 4 if low == 0 and padded >= 16 else 2) for low, _, padded in parts]
    cfg = dict(n=n, n_section=n_section, parts=parts, cuts=cuts, weight_cuts=cuts[0],
               final_cuts=column_cuts(width, 7))
    hbm = pl.BlockSpec(memory_space=pltpu.HBM)
    vmem = pl.BlockSpec(memory_space=pltpu.VMEM)
    dma = pltpu.SemaphoreType.DMA
    scratch = [
        pltpu.VMEM((tok, width), BF),
        pltpu.VMEM((tok, hidden_width), BF),
        pltpu.VMEM((hidden_width, width), BF),
        pltpu.VMEM((experts, tok), F32),
        pltpu.VMEM((experts, tok), F32),
        pltpu.VMEM((1, tok), jnp.int32),
        pltpu.VMEM((1, tok), jnp.int32),
        pltpu.SMEM(counts.shape[1:], jnp.int32),
    ]
    scratch += [pltpu.VMEM((n, padded, width), BF) for _, _, padded in parts]
    scratch += [pltpu.VMEM((n, padded, width), BF) for _, _, padded in parts]
    scratch += [pltpu.VMEM((n * padded, hidden_width), F32) for _, _, padded in parts]
    scratch += [pltpu.VMEM((n, padded, hidden_width), BF) for _, _, padded in parts]
    scratch += [pltpu.VMEM((n, padded, hidden_width), BF) for _, _, padded in parts]
    scratch += [pltpu.VMEM((n * padded, hidden_width), F32) for _, _, padded in parts]
    scratch += [dma((6,)), dma((cuts[0][0],)), dma((cfg["weight_cuts"][0],)), dma((4,))]
    scratch += [dma((n, count)) for count, _ in cuts]
    scratch += [dma((n, count)) for count, _ in cuts]
    scratch += [dma((n,)) for _ in cuts]
    scratch += [dma((n,)) for _ in cuts]
    kept = 2 * tok * (hidden_width + width) + 8 * tok * experts + 2 * experts * width
    vmem_limit = (67043328 - kept - 128 * 1024) // 4096 * 4096
    held = pl.pallas_call(
        functools.partial(kernel, cfg),
        out_shape=(
            pltpu.VMEM((1, tok, hidden_width), BF),
            pltpu.VMEM((1, experts, tok), F32),
            pltpu.VMEM((tok, width), BF),
            pltpu.VMEM((experts, tok), F32),
            pltpu.VMEM(router.shape, BF),
        ),
        in_specs=[hbm] * 8,
        out_specs=(vmem,) * 5,
        scratch_shapes=scratch,
        compiler_params=pltpu.CompilerParams(
            collective_id=0, has_side_effects=True, vmem_limit_bytes=vmem_limit),
    )(grad_out, hidden_act, jnp.swapaxes(scores, 1, 2), expert_ids, slot_ids, counts, down_weight, router)
    act_grad, score_grad, upstream = pl.pallas_call(
        functools.partial(finish_kernel, cfg),
        out_shape=(
            jax.ShapeDtypeStruct((1, tok, hidden_width), BF),
            jax.ShapeDtypeStruct((1, experts, tok), F32),
            jax.ShapeDtypeStruct((1, tok, width), BF),
        ),
        in_specs=[vmem] * 5,
        out_specs=(hbm,) * 3,
        scratch_shapes=[pltpu.VMEM((tok, width), BF), dma((cfg["final_cuts"][0] + 2,))],
        compiler_params=pltpu.CompilerParams(vmem_limit_bytes=16 * 1024 * 1024),
    )(*held)
    return act_grad, jnp.swapaxes(score_grad, 1, 2), upstream


def solution(mesh):
    in_specs = (
        P("section", "expert", None),
        P("section", "expert", None),
        P("section", "expert", None),
        P("section", "expert"),
        P("section", "expert"),
        P("section", None, None),
        P("expert", None, None),
        P(),
    )
    out_specs = (
        P("section", "expert", None),
        P("section", "expert", None),
        P("section", "expert", None),
    )
    return jax.shard_map(
        on_device, mesh=mesh, in_specs=in_specs, out_specs=out_specs, check_vma=False
    )
```

profile of v0, /device:TPU:0, one launch (start us, length us, event | category | flops | bytes accessed | tf_op | source)
XLA Modules:
  0.0 32.9 jit_solution(3958126684450428829)
XLA Ops:
  0.6 31.0 %shard_map.103 = (bf16[1,128,1024]{2,1,0:T(8,128)(2,1)S(1)}, f32[1,4,128]{2,1,0:T(4,128)S(1)}, bf16[128,3584]{1,0:T(8,128)(2,1)S(1)}, f32[4,128]{1,0:T(4,128)S(1)}, bf16[4,3584]{1,0:T(4,128)(2,1)S(1)}) custom-call(bf16[1,128,3584]{2,1,0:T(8,128)(2,1)} %grad_hbm.1, bf16[1,128,1024]{2,1,0:T(8,128)(2,1)} %hidden_hbm.1, f32[1,4,128]{2,1,0:T(4,128)} %bitcast.2, ...), custom_call_target="tpu_custom_call" | custom-call | tf_op jit(solution)/shard_map/pallas_call | solution.py:293
  31.7 1.2 %shard_map.104 = (bf16[1,128,1024]{2,1,0:T(8,128)(2,1)}, f32[1,4,128]{2,1,0:T(4,128)}, bf16[1,128,3584]{2,1,0:T(8,128)(2,1)}) custom-call(bf16[1,128,1024]{2,1,0:T(8,128)(2,1)S(1)} %get-tuple-element.11.act_in, f32[1,4,128]{2,1,0:T(4,128)S(1)} %get-tuple-element.12.score_in, bf16[128,3584]{1,0:T(8,128)(2,1)S(1)} %get-tuple-element.13.got, ...), custom_call_target="tpu_custom_call" | custom-call | tf_op jit(solution)/shard_map/pallas_call | solution.py:308
where the time goes:
time: 33 us; the launch traced here: 32.9 us
  Pallas kernels  32.2 us (98%)
  between operations  0.64 us (2%)
    pallas_call x1, Pallas kernels, on_device(): pl.pallas_call(functools.partial(kernel, cfg), out_shape=(pltpu.VMEM((1,...  31 us
    pallas_call x1, Pallas kernels, on_device(): pl.pallas_call(functools.partial(finish_kernel, cfg), out_shape=(jax.Shap...  1.21 us

commit v1 on v0

--- a/solution.py
+++ b/solution.py
@@ -33,26 +33,45 @@
     return pieces, width // pieces
 
 
-def kernel(cfg, grad_hbm, hidden_hbm, logits_hbm, ids_hbm, slots_hbm, counts_hbm, weight_hbm, router_hbm,
-           act_ref, score_ref, got, got_slope, router_ref, *rest):
+def kernel(cfg, *refs):
+    n_parts = len(cfg["parts"])
+    counts = [count for count, _ in cfg["cuts"]]
+    sizes = [6, counts[0], cfg["weight_cuts"][0], 4, n_parts, n_parts, n_parts] + counts
+    pl.run_scoped(
+        lambda *sems: exchange(cfg, refs[:8], refs[8:13], refs[13:], sems),
+        *[pltpu.SemaphoreType.DMA((size,)) for size in sizes])
+
+
+def exchange(cfg, inputs, outputs, scratch, sems):
+    grad_hbm, hidden_hbm, logits_hbm, ids_hbm, slots_hbm, counts_hbm, weight_hbm, router_hbm = inputs
+    act_ref, score_ref, got, got_slope, router_ref = outputs
     n, n_section, parts, cuts = cfg["n"], cfg["n_section"], cfg["parts"], cfg["cuts"]
     n_parts = len(parts)
-    rest = list(rest)
+    rest = list(scratch)
     take = lambda count: [rest.pop(0) for _ in range(count)]
     grad, hidden, weight, slope_out = take(4)
     logits_ref, ids_ref, slots_ref, counts_ref = take(4)
     sends, recvs, accs, results, returns, hiddens = (take(n_parts) for _ in range(6))
-    load_sem, grad_sem, weight_sem, up_sem = take(4)
-    send_sems, recv_sems, back_send, back_recv = (take(n_parts) for _ in range(4))
+    load_sem, grad_sem, weight_sem, up_sem, send_sem, back_send, back_recv = sems[:7]
+    recv_sems = sems[7:]
 
     tok, width = grad.shape
     section = lax.axis_index("section")
     me = lax.axis_index("expert")
     chips = n // 2
     chip, core = me // 2, lax.rem(me, 2)
-    target = [2 * lax.rem(chip + k // 2, chips) + lax.rem(core + k % 2, 2) for k in range(n)]
-    source = [2 * lax.rem(chip + chips - k // 2, chips) + lax.rem(core + k % 2, 2) for k in range(n)]
-    order = [k for k in range(2, n)] + [1]
+
+    def peer(k, sign):
+        far = k // 2
+        return 2 * lax.rem(chip + chips + sign * far, chips) + (k % 2 if far else lax.rem(core + k, 2))
+
+    def landing(k):
+        return 2 * (k // 2) + core if k // 2 else k
+
+    target = [peer(k, 1) for k in range(n)]
+    source = [peer(k, -1) for k in range(n)]
+    early = [k for k in range(2, n) if k % 2 == 0]
+    late = [k for k in range(2, n) if k % 2] + [1]
     has_prev, has_next = section > 0, section < n_section - 1
 
     pairs = [
@@ -113,8 +132,29 @@
     grad_up = pltpu.make_async_remote_copy(
         src_ref=grad, dst_ref=got, send_sem=up_sem.at[0], recv_sem=up_sem.at[1],
         device_id=(section - 1, me), device_id_type=MESH)
-
-    dispatch = {}
+    slope_up = pltpu.make_async_remote_copy(
+        src_ref=slope_out, dst_ref=got_slope, send_sem=up_sem.at[2], recv_sem=up_sem.at[3],
+        device_id=(section - 1, me), device_id_type=MESH)
+
+    def dispatch(p, k, span, sem):
+        return pltpu.make_async_remote_copy(
+            src_ref=sends[p].at[k, :, span], dst_ref=recvs[p].at[landing(k), :, span],
+            send_sem=send_sem.at[p], recv_sem=sem,
+            device_id=(section, target[k]), device_id_type=MESH)
+
+    def give_back(p, k):
+        return pltpu.make_async_remote_copy(
+            src_ref=results[p].at[k], dst_ref=returns[p].at[landing(k)],
+            send_sem=back_send.at[p], recv_sem=back_recv.at[p],
+            device_id=(section, source[k]), device_id_type=MESH)
+
+    def all_of(src, dst, send, recv):
+        return pltpu.make_async_remote_copy(
+            src_ref=src, dst_ref=dst, send_sem=send, recv_sem=recv,
+            device_id=(section, target[1]), device_id_type=MESH)
+
+    others = pl.ds(1, n - 1)
+    barred = True
     for p, (low, high, padded) in enumerate(parts):
         count, cols = cuts[p]
         pick = picks[p].astype(BF)
@@ -126,15 +166,11 @@
             block = block.reshape(n, padded, cols)
             sends[p][:, :, span] = block
             recvs[p][0, :, span] = block[0]
-            if not dispatch:
+            if barred:
                 pl.semaphore_wait(barrier, n - 1 + jnp.where(has_prev, 1, 0) + jnp.where(has_next, 1, 0))
-            for k in order:
-                copy = pltpu.make_async_remote_copy(
-                    src_ref=sends[p].at[k, :, span], dst_ref=recvs[p].at[k, :, span],
-                    send_sem=send_sems[p].at[k, c], recv_sem=recv_sems[p].at[k, c],
-                    device_id=(section, target[k]), device_id_type=MESH)
-                copy.start()
-                dispatch[p, c, k] = copy
+                barred = False
+            for k in early + late:
+                dispatch(p, k, span, recv_sems[p].at[c]).start()
         if p == 0:
 
             @pl.when(has_prev)
@@ -157,8 +193,8 @@
     for p in range(n_parts):
         hiddens[p][...] = jnp.dot(picks[p].astype(BF), hidden[...], preferred_element_type=F32)
 
-    backs = {}
     weights_waited = 0
+    held = []
     for p, (low, high, padded) in enumerate(parts):
         count, cols = cuts[p]
         rows = n * padded
@@ -166,9 +202,9 @@
             while weights_waited * weight_cols < (c + 1) * cols:
                 weight_loads[weights_waited].wait()
                 weights_waited += 1
-            for k in range(1, n):
-                dispatch[p, c, k].wait_recv()
             span = pl.ds(c * cols, cols)
+            all_of(sends[p].at[others, :, span], recvs[p].at[others, :, span],
+                   send_sem.at[p], recv_sems[p].at[c]).wait_recv()
             part = lax.dot_general(
                 recvs[p][:, :, span].reshape(rows, cols), weight[:, span],
                 (((1,), (1,)), ((), ())), preferred_element_type=F32)
@@ -179,28 +215,24 @@
         done = part.astype(BF).reshape(n, padded, part.shape[1])
         results[p][...] = done
         returns[p][0] = done[0]
-        for k in order:
-            copy = pltpu.make_async_remote_copy(
-                src_ref=results[p].at[k], dst_ref=returns[p].at[k],
-                send_sem=back_send[p].at[k], recv_sem=back_recv[p].at[k],
-                device_id=(section, source[k]), device_id_type=MESH)
-            copy.start()
-            backs[p, k] = copy
+        for k in early:
+            give_back(p, k).start()
+        held += [(p, k) for k in late]
+        if p in (0, n_parts - 1):
+            for q, k in held:
+                give_back(q, k).start()
+            held = []
 
     route_grad = jnp.zeros((1, tok), F32)
     for p, (low, high, padded) in enumerate(parts):
         rows = n * padded
-        for k in range(1, n):
-            backs[p, k].wait_recv()
+        all_of(results[p].at[others], returns[p].at[others], back_send.at[p], back_recv.at[p]).wait_recv()
         own = returns[p][...].reshape(rows, returns[p].shape[2]).astype(F32)
         by_row = jnp.sum(hiddens[p][...] * own, axis=1, keepdims=True)
         route_grad += jnp.sum(jnp.where(picks[p], by_row, 0.0), axis=0, keepdims=True)
     slope = route_grad * route_scale * sigmoid_vals * (1.0 - sigmoid_vals)
     slopes = jnp.where(onehot, slope, 0.0)
     slope_out[...] = slopes
-    slope_up = pltpu.make_async_remote_copy(
-        src_ref=slope_out, dst_ref=got_slope, send_sem=up_sem.at[2], recv_sem=up_sem.at[3],
-        device_id=(section - 1, me), device_id_type=MESH)
 
     @pl.when(has_prev)
     def _():
@@ -216,42 +248,42 @@
         own_back = term if own_back is None else own_back + term
     act_ref[0] = (gate * own_back).astype(BF)
 
-    for copy in list(dispatch.values()) + list(backs.values()):
-        copy.wait_send()
+    for p in range(n_parts):
+        all_of(sends[p].at[others], recvs[p].at[others], send_sem.at[p], recv_sems[p].at[0]).wait_send()
+        all_of(results[p].at[others], returns[p].at[others], back_send.at[p], back_recv.at[p]).wait_send()
 
     @pl.when(has_prev)
     def _():
         grad_up.wait_send()
+        slope_up.wait_send()
 
     @pl.when(has_next)
     def _():
         grad_up.wait_recv()
         slope_up.wait_recv()
 
-    @pl.when(has_prev)
-    def _():
-        slope_up.wait_send()
-
-
-def finish_kernel(cfg, act_in, score_in, got, got_slope, router_ref, act_out, score_out, up_out, up, sems):
-    count, cols = cfg["final_cuts"]
-    act_copy = pltpu.make_async_copy(act_in, act_out, sems.at[count])
-    score_copy = pltpu.make_async_copy(score_in, score_out, sems.at[count + 1])
-    act_copy.start()
-    score_copy.start()
-    is_last = lax.axis_index("section") == cfg["n_section"] - 1
-    scores_bf = got_slope[...].astype(BF)
-    copies = []
-    for c in range(count):
-        span = pl.ds(c * cols, cols)
-        term = lax.dot_general(
-            scores_bf, router_ref[:, span], (((0,), (0,)), ((), ())), preferred_element_type=F32)
-        token_grad = got[:, span].astype(F32) + term
-        up[:, span] = jnp.where(is_last, 0.0, token_grad).astype(BF)
-        copies.append(pltpu.make_async_copy(up.at[:, span], up_out.at[0, :, span], sems.at[c]))
-        copies[-1].start()
-    for copy in copies + [act_copy, score_copy]:
-        copy.wait()
+
+def finish_kernel(cfg, act_in, score_in, got, got_slope, router_ref, act_out, score_out, up_out, up):
+    def scoped(sems):
+        count, cols = cfg["final_cuts"]
+        copies = [pltpu.make_async_copy(act_in, act_out, sems.at[0]),
+                  pltpu.make_async_copy(score_in, score_out, sems.at[1]),
+                  pltpu.make_async_copy(up, up_out.at[0], sems.at[2])]
+        for copy in copies[:2]:
+            copy.start()
+        is_last = lax.axis_index("section") == cfg["n_section"] - 1
+        scores_bf = got_slope[...].astype(BF)
+        for c in range(count):
+            span = pl.ds(c * cols, cols)
+            term = lax.dot_general(
+                scores_bf, router_ref[:, span], (((0,), (0,)), ((), ())), preferred_element_type=F32)
+            token_grad = got[:, span].astype(F32) + term
+            up[:, span] = jnp.where(is_last, 0.0, token_grad).astype(BF)
+            pltpu.make_async_copy(up.at[:, span], up_out.at[0, :, span], sems.at[2]).start()
+        for copy in copies:
+            copy.wait()
+
+    pl.run_scoped(scoped, pltpu.SemaphoreType.DMA((3,)))
 
 
 def on_device(grad_out, hidden_act, scores, expert_ids, slot_ids, counts, down_weight, router):
@@ -261,12 +293,11 @@
     experts = scores.shape[2]
     capacity = max(2, 7 * tok // (4 * n))
     parts = row_parts(capacity)
-    cuts = [column_cuts(width, 4 if low == 0 and padded >= 16 else 2) for low, _, padded in parts]
-    cfg = dict(n=n, n_section=n_section, parts=parts, cuts=cuts, weight_cuts=cuts[0],
+    cuts = [column_cuts(width, 2 if low and padded >= 16 else 4) for low, _, padded in parts]
+    cfg = dict(n=n, n_section=n_section, parts=parts, cuts=cuts, weight_cuts=column_cuts(width, 4),
                final_cuts=column_cuts(width, 7))
     hbm = pl.BlockSpec(memory_space=pltpu.HBM)
     vmem = pl.BlockSpec(memory_space=pltpu.VMEM)
-    dma = pltpu.SemaphoreType.DMA
     scratch = [
         pltpu.VMEM((tok, width), BF),
         pltpu.VMEM((tok, hidden_width), BF),
@@ -283,11 +314,6 @@
     scratch += [pltpu.VMEM((n, padded, hidden_width), BF) for _, _, padded in parts]
     scratch += [pltpu.VMEM((n, padded, hidden_width), BF) for _, _, padded in parts]
     scratch += [pltpu.VMEM((n * padded, hidden_width), F32) for _, _, padded in parts]
-    scratch += [dma((6,)), dma((cuts[0][0],)), dma((cfg["weight_cuts"][0],)), dma((4,))]
-    scratch += [dma((n, count)) for count, _ in cuts]
-    scratch += [dma((n, count)) for count, _ in cuts]
-    scratch += [dma((n,)) for _ in cuts]
-    scratch += [dma((n,)) for _ in cuts]
     kept = 2 * tok * (hidden_width + width) + 8 * tok * experts + 2 * experts * width
     vmem_limit = (67043328 - kept - 128 * 1024) // 4096 * 4096
     held = pl.pallas_call(
@@ -314,7 +340,7 @@
         ),
         in_specs=[vmem] * 5,
         out_specs=(hbm,) * 3,
-        scratch_shapes=[pltpu.VMEM((tok, width), BF), dma((cfg["final_cuts"][0] + 2,))],
+        scratch_shapes=[pltpu.VMEM((tok, width), BF)],
         compiler_params=pltpu.CompilerParams(vmem_limit_bytes=16 * 1024 * 1024),
     )(*held)
     return act_grad, jnp.swapaxes(score_grad, 1, 2), upstream

time: 33 us -> 31.3 us (0.948)
  Pallas kernels: 32.2 us -> 30.5 us
    pallas_call x1, Pallas kernels: 31 us -> 29.4 us  [on_device(): pl.pallas_call(functools.partial(kernel, cfg), out_shape=(pltpu.VMEM((1,...]
where the time goes in v1:
time: 31.3 us; the launch traced here: 31.1 us
  Pallas kernels  30.5 us (97%)
  between operations  0.63 us (2%)
    pallas_call x1, Pallas kernels, on_device(): pl.pallas_call(functools.partial(kernel, cfg), out_shape=(pltpu.VMEM((1,...  29.4 us
    pallas_call x1, Pallas kernels, on_device(): pl.pallas_call(functools.partial(finish_kernel, cfg), out_shape=(jax.Shap...  1.13 us

profile of v1, /device:TPU:0, one launch (start us, length us, event | category | flops | bytes accessed | tf_op | source)
XLA Modules:
  0.0 31.1 jit_solution(8711750464586668788)
XLA Ops:
  0.6 29.4 %shard_map.103 = (bf16[1,128,1024]{2,1,0:T(8,128)(2,1)S(1)}, f32[1,4,128]{2,1,0:T(4,128)S(1)}, bf16[128,3584]{1,0:T(8,128)(2,1)S(1)}, f32[4,128]{1,0:T(4,128)S(1)}, bf16[4,3584]{1,0:T(4,128)(2,1)S(1)}) custom-call(bf16[1,128,3584]{2,1,0:T(8,128)(2,1)} %refs_0_.1, bf16[1,128,1024]{2,1,0:T(8,128)(2,1)} %refs_1_.1, f32[1,4,128]{2,1,0:T(4,128)} %bitcast.2, ...), custom_call_target="tpu_custom_call" | custom-call | tf_op jit(solution)/shard_map/pallas_call | solution.py:319
  30.0 1.1 %shard_map.104 = (bf16[1,128,1024]{2,1,0:T(8,128)(2,1)}, f32[1,4,128]{2,1,0:T(4,128)}, bf16[1,128,3584]{2,1,0:T(8,128)(2,1)}) custom-call(bf16[1,128,1024]{2,1,0:T(8,128)(2,1)S(1)} %get-tuple-element.11.act_in, f32[1,4,128]{2,1,0:T(4,128)S(1)} %get-tuple-element.12.score_in, bf16[128,3584]{1,0:T(8,128)(2,1)S(1)} %get-tuple-element.13.got, ...), custom_call_target="tpu_custom_call" | custom-call | tf_op jit(solution)/shard_map/pallas_call | solution.py:334

commit v2 on v1

--- a/solution.py
+++ b/solution.py
@@ -17,14 +17,18 @@
     head = capacity // 16 * 16
     if head == capacity and head >= 32:
         head -= 16
-    parts = []
-    if head > 16:
-        parts.append((0, head - 16, head - 16))
-    if head:
-        parts.append((max(head - 16, 0), head, 16))
+    parts = [(0, head, head)] if head else []
     if capacity > head:
         parts.append((head, capacity, -(-(capacity - head) // 8) * 8))
     return parts
+
+
+def row_pieces(parts):
+    pieces = []
+    for p, (low, high, padded) in enumerate(parts):
+        edges = [0, 16, padded] if p == 0 and len(parts) > 1 and padded > 16 else [0, padded]
+        pieces += [(p, first, last) for first, last in zip(edges[:-1], edges[1:])]
+    return pieces
 
 
 def column_cuts(width, pieces):
@@ -34,9 +38,9 @@
 
 
 def kernel(cfg, *refs):
-    n_parts = len(cfg["parts"])
+    n_parts, n_pieces = len(cfg["parts"]), len(cfg["pieces"])
     counts = [count for count, _ in cfg["cuts"]]
-    sizes = [6, counts[0], cfg["weight_cuts"][0], 4, n_parts, n_parts, n_parts] + counts
+    sizes = [6, counts[0], cfg["weight_cuts"][0], 4, n_parts, n_pieces, n_pieces] + counts
     pl.run_scoped(
         lambda *sems: exchange(cfg, refs[:8], refs[8:13], refs[13:], sems),
         *[pltpu.SemaphoreType.DMA((size,)) for size in sizes])
@@ -46,12 +50,14 @@
     grad_hbm, hidden_hbm, logits_hbm, ids_hbm, slots_hbm, counts_hbm, weight_hbm, router_hbm = inputs
     act_ref, score_ref, got, got_slope, router_ref = outputs
     n, n_section, parts, cuts = cfg["n"], cfg["n_section"], cfg["parts"], cfg["cuts"]
-    n_parts = len(parts)
+    pieces = cfg["pieces"]
+    n_parts, n_pieces = len(parts), len(pieces)
     rest = list(scratch)
     take = lambda count: [rest.pop(0) for _ in range(count)]
     grad, hidden, weight, slope_out = take(4)
     logits_ref, ids_ref, slots_ref, counts_ref = take(4)
-    sends, recvs, accs, results, returns, hiddens = (take(n_parts) for _ in range(6))
+    sends, recvs, accs = (take(n_parts) for _ in range(3))
+    results, returns, hiddens = (take(n_pieces) for _ in range(3))
     load_sem, grad_sem, weight_sem, up_sem, send_sem, back_send, back_recv = sems[:7]
     recv_sems = sems[7:]
 
@@ -71,7 +77,7 @@
     target = [peer(k, 1) for k in range(n)]
     source = [peer(k, -1) for k in range(n)]
     early = [k for k in range(2, n) if k % 2 == 0]
-    late = [k for k in range(2, n) if k % 2] + [1]
+    late = [k for k in range(2, n) if k % 2]
     has_prev, has_next = section > 0, section < n_section - 1
 
     pairs = [
@@ -87,7 +93,17 @@
         )
         for c in range(cuts[0][0])
     ]
-    for load in loads[:3] + grad_loads + loads[3:]:
+    for load in loads[:3] + grad_loads[:1]:
+        load.start()
+    barrier = pltpu.get_barrier_semaphore()
+    for k in range(1, n):
+        pl.semaphore_signal(barrier, inc=1, device_id=(section, target[k]), device_id_type=MESH)
+
+    @pl.when(has_next)
+    def _():
+        pl.semaphore_signal(barrier, inc=1, device_id=(section + 1, me), device_id_type=MESH)
+
+    for load in grad_loads[1:] + loads[3:]:
         load.start()
     weight_cuts, weight_cols = cfg["weight_cuts"]
     weight_loads = [
@@ -98,18 +114,6 @@
         )
         for c in range(weight_cuts)
     ]
-
-    barrier = pltpu.get_barrier_semaphore()
-    for k in range(1, n):
-        pl.semaphore_signal(barrier, inc=1, device_id=(section, target[k]), device_id_type=MESH)
-
-    @pl.when(has_prev)
-    def _():
-        pl.semaphore_signal(barrier, inc=1, device_id=(section - 1, me), device_id_type=MESH)
-
-    @pl.when(has_next)
-    def _():
-        pl.semaphore_signal(barrier, inc=1, device_id=(section + 1, me), device_id_type=MESH)
 
     for load in loads[:3]:
         load.wait()
@@ -122,11 +126,12 @@
         limit = jnp.where(here, counts_ref[me, target[k]], limit)
         slot_of = jnp.where(here, k, slot_of)
     live = places < limit
-    picks = []
-    for low, high, padded in parts:
+
+    def picked(low, high, padded):
         inside = live & (places >= low) & (places < high)
         goal = jnp.where(inside, slot_of * padded + places - low, -1)
-        picks.append(lax.broadcasted_iota(jnp.int32, (n * padded, tok), 0) == goal)
+        return lax.broadcasted_iota(jnp.int32, (n * padded, tok), 0) == goal
+
     eye = lax.broadcasted_iota(jnp.int32, (tok, tok), 0) == lax.broadcasted_iota(jnp.int32, (tok, tok), 1)
 
     grad_up = pltpu.make_async_remote_copy(
@@ -142,10 +147,10 @@
             send_sem=send_sem.at[p], recv_sem=sem,
             device_id=(section, target[k]), device_id_type=MESH)
 
-    def give_back(p, k):
+    def give_back(q, k):
         return pltpu.make_async_remote_copy(
-            src_ref=results[p].at[k], dst_ref=returns[p].at[landing(k)],
-            send_sem=back_send.at[p], recv_sem=back_recv.at[p],
+            src_ref=results[q].at[k], dst_ref=returns[q].at[landing(k)],
+            send_sem=back_send.at[q], recv_sem=back_recv.at[q],
             device_id=(section, source[k]), device_id_type=MESH)
 
     def all_of(src, dst, send, recv):
@@ -157,7 +162,7 @@
     barred = True
     for p, (low, high, padded) in enumerate(parts):
         count, cols = cuts[p]
-        pick = picks[p].astype(BF)
+        pick = picked(low, high, padded).astype(BF)
         for c in range(count):
             span = pl.ds(c * cols, cols)
             if p == 0:
@@ -167,9 +172,9 @@
             sends[p][:, :, span] = block
             recvs[p][0, :, span] = block[0]
             if barred:
-                pl.semaphore_wait(barrier, n - 1 + jnp.where(has_prev, 1, 0) + jnp.where(has_next, 1, 0))
+                pl.semaphore_wait(barrier, n - 1 + jnp.where(has_prev, 1, 0))
                 barred = False
-            for k in early + late:
+            for k in early + late + [1]:
                 dispatch(p, k, span, recv_sems[p].at[c]).start()
         if p == 0:
 
@@ -190,8 +195,9 @@
     chosen_logit = jnp.sum(jnp.where(onehot, logits, 0.0), axis=0, keepdims=True)
     sigmoid_vals = jax.nn.sigmoid(chosen_logit)
     gate = upright((route_scale * sigmoid_vals).astype(BF).astype(F32))
-    for p in range(n_parts):
-        hiddens[p][...] = jnp.dot(picks[p].astype(BF), hidden[...], preferred_element_type=F32)
+    picks = [picked(parts[p][0] + first, parts[p][0] + last, last - first) for p, first, last in pieces]
+    for q in range(n_pieces):
+        hiddens[q][...] = jnp.dot(picks[q].astype(BF), hidden[...], preferred_element_type=F32)
 
     weights_waited = 0
     held = []
@@ -213,23 +219,25 @@
             if c < count - 1:
                 accs[p][...] = part
         done = part.astype(BF).reshape(n, padded, part.shape[1])
-        results[p][...] = done
-        returns[p][0] = done[0]
-        for k in early:
-            give_back(p, k).start()
-        held += [(p, k) for k in late]
-        if p in (0, n_parts - 1):
-            for q, k in held:
-                give_back(q, k).start()
-            held = []
+        for q, (of, first, last) in enumerate(pieces):
+            if of == p:
+                results[q][...] = done[:, first:last]
+                returns[q][0] = done[0, first:last]
+                give_back(q, 1).start()
+                for k in early:
+                    give_back(q, k).start()
+                held += [(q, k) for k in late]
+        rush = 1 if p < n_parts - 1 else n_pieces
+        for q, k in [(q, k) for q, k in held if q < rush]:
+            give_back(q, k).start()
+        held = [(q, k) for q, k in held if q >= rush]
 
     route_grad = jnp.zeros((1, tok), F32)
-    for p, (low, high, padded) in enumerate(parts):
-        rows = n * padded
-        all_of(results[p].at[others], returns[p].at[others], back_send.at[p], back_recv.at[p]).wait_recv()
-        own = returns[p][...].reshape(rows, returns[p].shape[2]).astype(F32)
-        by_row = jnp.sum(hiddens[p][...] * own, axis=1, keepdims=True)
-        route_grad += jnp.sum(jnp.where(picks[p], by_row, 0.0), axis=0, keepdims=True)
+    for q in range(n_pieces):
+        all_of(results[q].at[others], returns[q].at[others], back_send.at[q], back_recv.at[q]).wait_recv()
+        own = returns[q][...].reshape(hiddens[q].shape).astype(F32)
+        by_row = jnp.sum(hiddens[q][...] * own, axis=1, keepdims=True)
+        route_grad += jnp.sum(jnp.where(picks[q], by_row, 0.0), axis=0, keepdims=True)
     slope = route_grad * route_scale * sigmoid_vals * (1.0 - sigmoid_vals)
     slopes = jnp.where(onehot, slope, 0.0)
     slope_out[...] = slopes
@@ -240,17 +248,22 @@
 
     score_ref[0] = slopes
     own_back = None
-    for p, (low, high, padded) in enumerate(parts):
-        rows = n * padded
+    for q in range(n_pieces):
         term = lax.dot_general(
-            picks[p].astype(BF), returns[p][...].reshape(rows, returns[p].shape[2]),
+            picks[q].astype(BF), returns[q][...].reshape(hiddens[q].shape),
             (((0,), (0,)), ((), ())), preferred_element_type=F32)
         own_back = term if own_back is None else own_back + term
     act_ref[0] = (gate * own_back).astype(BF)
 
+    @pl.when(jnp.logical_not(has_next))
+    def _():
+        got[...] = jnp.zeros_like(got)
+        got_slope[...] = jnp.zeros_like(got_slope)
+
     for p in range(n_parts):
         all_of(sends[p].at[others], recvs[p].at[others], send_sem.at[p], recv_sems[p].at[0]).wait_send()
-        all_of(results[p].at[others], returns[p].at[others], back_send.at[p], back_recv.at[p]).wait_send()
+    for q in range(n_pieces):
+        all_of(results[q].at[others], returns[q].at[others], back_send.at[q], back_recv.at[q]).wait_send()
 
     @pl.when(has_prev)
     def _():
@@ -271,14 +284,13 @@
                   pltpu.make_async_copy(up, up_out.at[0], sems.at[2])]
         for copy in copies[:2]:
             copy.start()
-        is_last = lax.axis_index("section") == cfg["n_section"] - 1
         scores_bf = got_slope[...].astype(BF)
         for c in range(count):
             span = pl.ds(c * cols, cols)
             term = lax.dot_general(
                 scores_bf, router_ref[:, span], (((0,), (0,)), ((), ())), preferred_element_type=F32)
             token_grad = got[:, span].astype(F32) + term
-            up[:, span] = jnp.where(is_last, 0.0, token_grad).astype(BF)
+            up[:, span] = token_grad.astype(BF)
             pltpu.make_async_copy(up.at[:, span], up_out.at[0, :, span], sems.at[2]).start()
         for copy in copies:
             copy.wait()
@@ -293,8 +305,9 @@
     experts = scores.shape[2]
     capacity = max(2, 7 * tok // (4 * n))
     parts = row_parts(capacity)
-    cuts = [column_cuts(width, 2 if low and padded >= 16 else 4) for low, _, padded in parts]
-    cfg = dict(n=n, n_section=n_section, parts=parts, cuts=cuts, weight_cuts=column_cuts(width, 4),
+    pieces = row_pieces(parts)
+    cuts = [column_cuts(width, 7) for _ in parts]
+    cfg = dict(n=n, n_section=n_section, parts=parts, pieces=pieces, cuts=cuts, weight_cuts=column_cuts(width, 7),
                final_cuts=column_cuts(width, 7))
     hbm = pl.BlockSpec(memory_space=pltpu.HBM)
     vmem = pl.BlockSpec(memory_space=pltpu.VMEM)
@@ -311,9 +324,9 @@
     scratch += [pltpu.VMEM((n, padded, width), BF) for _, _, padded in parts]
     scratch += [pltpu.VMEM((n, padded, width), BF) for _, _, padded in parts]
     scratch += [pltpu.VMEM((n * padded, hidden_width), F32) for _, _, padded in parts]
-    scratch += [pltpu.VMEM((n, padded, hidden_width), BF) for _, _, padded in parts]
-    scratch += [pltpu.VMEM((n, padded, hidden_width), BF) for _, _, padded in parts]
-    scratch += [pltpu.VMEM((n * padded, hidden_width), F32) for _, _, padded in parts]
+    scratch += [pltpu.VMEM((n, last - first, hidden_width), BF) for _, first, last in pieces]
+    scratch += [pltpu.VMEM((n, last - first, hidden_width), BF) for _, first, last in pieces]
+    scratch += [pltpu.VMEM((n * (last - first), hidden_width), F32) for _, first, last in pieces]
     kept = 2 * tok * (hidden_width + width) + 8 * tok * experts + 2 * experts * width
     vmem_limit = (67043328 - kept - 128 * 1024) // 4096 * 4096
     held = pl.pallas_call(

time: 31.3 us -> 30.9 us (0.987)
  Pallas kernels: 30.5 us -> 30.1 us
    pallas_call x1, Pallas kernels: 29.4 us -> 29 us  [on_device(): pl.pallas_call(functools.partial(kernel, cfg), out_shape=(pltpu.VMEM((1,...]
where the time goes in v2:
time: 30.9 us; the launch traced here: 30.7 us
  Pallas kernels  30.1 us (97%)
  between operations  0.63 us (2%)
    pallas_call x1, Pallas kernels, on_device(): pl.pallas_call(functools.partial(kernel, cfg), out_shape=(pltpu.VMEM((1,...  29 us
    pallas_call x1, Pallas kernels, on_device(): pl.pallas_call(functools.partial(finish_kernel, cfg), out_shape=(jax.Shap...  1.13 us

profile of v2, /device:TPU:0, one launch (start us, length us, event | category | flops | bytes accessed | tf_op | source)
XLA Modules:
  0.0 30.7 jit_solution(16044025435650996332)
XLA Ops:
  0.6 29.0 %shard_map.103 = (bf16[1,128,1024]{2,1,0:T(8,128)(2,1)S(1)}, f32[1,4,128]{2,1,0:T(4,128)S(1)}, bf16[128,3584]{1,0:T(8,128)(2,1)S(1)}, f32[4,128]{1,0:T(4,128)S(1)}, bf16[4,3584]{1,0:T(4,128)(2,1)S(1)}) custom-call(bf16[1,128,3584]{2,1,0:T(8,128)(2,1)} %refs_0_.1, bf16[1,128,1024]{2,1,0:T(8,128)(2,1)} %refs_1_.1, f32[1,4,128]{2,1,0:T(4,128)} %bitcast.2, ...), custom_call_target="tpu_custom_call" | custom-call | tf_op jit(solution)/shard_map/pallas_call | solution.py:332
  29.6 1.1 %shard_map.104 = (bf16[1,128,1024]{2,1,0:T(8,128)(2,1)}, f32[1,4,128]{2,1,0:T(4,128)}, bf16[1,128,3584]{2,1,0:T(8,128)(2,1)}) custom-call(bf16[1,128,1024]{2,1,0:T(8,128)(2,1)S(1)} %get-tuple-element.11.act_in, f32[1,4,128]{2,1,0:T(4,128)S(1)} %get-tuple-element.12.score_in, bf16[128,3584]{1,0:T(8,128)(2,1)S(1)} %get-tuple-element.13.got, ...), custom_call_target="tpu_custom_call" | custom-call | tf_op jit(solution)/shard_map/pallas_call | solution.py:347
